TPU v7x, 32 devices: a whole 2x2x4 slice. The times are simulated.
32 devices in a mesh: wide: 8 (over y, x, core), narrow: 4 (over z).
Axes of the slice: x: 2, y: 2, z: 4, core: 2. Of those that a mesh axis runs over, the one named last changes fastest.
Arguments:
- coefficients: float32 [8, 8192, 8192], P(None, 'wide', 'narrow'), may hold values from -0.07 to 0.07
- tensor_blocks: float32 [8, 32, 8192], P(None, 'wide', 'narrow'), may hold values from -6 to 6
- basis_rows: float32 [32, 8192], P(None, ('wide', 'narrow')), may hold values from -1.1 to 1.1, as said below
Outputs:
- new_basis: float32 [32, 8192], P(None, ('wide', 'narrow'))
- projection: float32 [32, 32], replicated
- factor: float32 [32, 32], replicated
Inputs may be any that keep to these rules, and one draw needn't show every extreme that they name: The rows of basis_rows are nearly but not exactly orthonormal: basis_rows basis_rows^T differs from the identity by less than 0.2 in spectral norm.
All inputs are finite; a program needn't handle non-finite values.
Results may differ from a plain program's by a relative error of at most 0.0002.
Values sent between devices are 32-bit elements; how exact they have to be, the bound alone decides.
A program may use at most 128 MiB of HBM per device.

v0:
```python
import jax
import jax.numpy as jnp
from jax import lax
from jax.sharding import PartitionSpec as P

N = 8192


def body(coefficients, tensor_blocks, basis_rows):
    hi = lax.Precision.HIGHEST
    partial_block = jnp.einsum(
        "kic,krc->ir",
        lax.all_gather(tensor_blocks, "wide", axis=1, tiled=True),
        coefficients,
        precision=hi,
    )
    image = lax.psum_scatter(partial_block, "narrow", scatter_dimension=1, tiled=True)
    local_first = jnp.dot(basis_rows, image.T, precision=hi)
    local_correlation = jnp.dot(basis_rows, basis_rows.T, precision=hi)
    first, correlation = lax.psum((local_first, local_correlation), ("wide", "narrow"))
    once = image - jnp.dot(first.T, basis_rows, precision=hi)
    second, raw_gram = lax.psum(
        (jnp.dot(basis_rows, once.T, precision=hi), jnp.dot(once, once.T, precision=hi)),
        ("wide", "narrow"),
    )
    twice = once - jnp.dot(second.T, basis_rows, precision=hi)
    cross = jnp.dot(second.T, second, precision=hi)
    weighted = jnp.dot(second.T, jnp.dot(correlation, second, precision=hi), precision=hi)
    gram = (raw_gram - 2.0 * cross + weighted) / N
    factor = jnp.linalg.cholesky(gram)
    new_basis = lax.linalg.triangular_solve(factor, twice, left_side=True, lower=True)
    return (new_basis, first + second, factor)


def solution(mesh):
    in_specs = (P(None, "wide", "narrow"), P(None, "wide", "narrow"), P(None, ("wide", "narrow")))
    out_specs = (P(None, ("wide", "narrow")), P(), P())
    return jax.shard_map(body, mesh=mesh, in_specs=in_specs, out_specs=out_specs, check_vma=False)
```

profile of v0, /device:TPU:0, one launch (start us, length us, event | category | flops | bytes accessed | tf_op | source)
XLA Modules:
  0.0 225.5 jit_solution(1987830653347588551)
XLA Ops:
  7.2 0.0 all-gather.2.cloned.1.call-start
  7.2 1.8 copy.11
  9.1 0.0 reduce-scatter.2.cloned.1.call-start
  9.1 31.3 %all-gather.2.cloned.1.call-done = f32[8,32,2048]{2,0,1:T(8,128)} async-done(((f32[8,4,2048]{2,0,1:T(8,128)}), f32[8,32,2048]{2,0,1:T(8,128)}) %all-gather.2.cloned.1.call-update) | async-done | bytes 2097168 | tf_op jit(solution)/shard_map/all_gather | solution.py:13
  40.4 67.1 %fusion.2 = f32[32,1024]{1,0:T(8,128)} fusion(f32[8,1024,2048]{2,1,0:T(8,128)} %param.3, f32[8,32,2048]{2,0,1:T(8,128)} %all-gather.2.cloned.1.call-done), kind=kOutput, calls=%fused_computation.2 | convolution fusion | flops 6442450944 | bytes 69337088 | tf_op jit(solution)/shard_map/kic,krc->ir/dot_general | solution.py:11
  107.5 0.2 fusion.11
  107.7 19.4 %reduce-scatter.2.cloned.1.call-done = f32[32,256]{1,0:T(8,128)} async-done(((f32[32,1024]{1,0:T(8,128)}), f32[32,256]{1,0:T(8,128)}) %reduce-scatter.2.cloned.1.call-update) | async-done | bytes 32784 | tf_op jit(solution)/shard_map/reduce_scatter | solution.py:17
  127.1 0.9 convolution_bitcast_fusion.1
  128.1 38.5 %psum.28 = f32[32,32]{0,1:T(8,128)S(1)} all-reduce(f32[32,32]{0,1:T(8,128)S(1)} %convolution_bitcast_fusion.1), channel_id=1, replica_groups=mesh['wide'=8,'narrow'=4] {'wide','narrow'}, use_global_device_ids=true, to_apply=%region_1.0 | all-reduce | flops 1024 | bytes 8192 | tf_op jit(solution)/shard_map/psum | solution.py:20
  166.5 0.9 convolution_subtract_fusion.1
  167.4 0.2 convolution_bitcast_fusion
  167.6 0.2 fusion.10
  167.8 41.3 %all-reduce = (f32[32,32]{0,1:T(8,128)S(1)}, f32[32,32]{0,1:T(8,128)S(1)}, f32[32,32]{1,0:T(8,128)S(1)}) all-reduce(f32[32,32]{0,1:T(8,128)S(1)} %convolution_bitcast_fusion, f32[32,32]{0,1:T(8,128)S(1)} %fusion.10, f32[32,32]{1,0:T(8,128)S(1)} %fusion.11), channel_id=1, replica_groups=mesh['wide'=8,'narrow'=4] {'wide','narrow'}, use_global_device_ids=true, to_apply=%region_3.0 | all-reduce | flops 3072 | bytes 24576 | tf_op jit(solution)/shard_map/psum | solution.py:22
  209.1 0.2 convolution_subtract_fusion
  209.2 0.1 fusion.12
  209.4 0.2 fusion.6
  209.6 0.2 fusion.5
  209.8 0.1 copy.16
  209.9 2.9 %cholesky.16 = f32[32,32]{1,0:T(8,128)S(1)} custom-call(f32[32,32]{1,0:T(8,128)S(1)} %fusion.9), custom_call_target="Cholesky" | custom-call | tf_op jit(solution)/shard_map/jit(cholesky)/cholesky | solution.py:30
  212.8 0.6 compare_reduce_fusion
  213.5 1.3 select_bitcast_fusion
  214.7 2.4 %custom-call.6 = f32[1,32,32]{1,2,0:T(8,128)S(1)} custom-call(f32[1,32,32]{2,1,0:T(8,128)S(1)} %get-tuple-element.12), custom_call_target="InvertDiagBlocksLowerTriangular" | custom-call | tf_op jit(solution)/shard_map/triangular_solve | solution.py:31
  217.1 0.7 copy.17
  217.9 0.8 fusion.7
  (7 shorter events, 0.1 us)
Async XLA Ops:
  7.2 100.4 %copy-start = (f32[32,256]{1,0:T(8,128)S(1)}, f32[32,256]{1,0:T(8,128)}, u32[]{:S(2)}) copy-start(f32[32,256]{1,0:T(8,128)} %param.5) | copy-start | bytes 98308
  7.2 33.2 %all-gather.2.cloned.1.call-start = ((), (), s32[]{:S(2)}) async-start(), calls=%async_computation.1 | async-start | bytes 2359296 | tf_op jit(solution)/shard_map/all_gather | solution.py:13
  9.1 118.1 %reduce-scatter.2.cloned.1.call-start = ((), (), s32[]{:S(2)}) async-start(), calls=%async_computation.2 | async-start | bytes 163840 | tf_op jit(solution)/shard_map/reduce_scatter | solution.py:17
Sparse Core Ops, SparseCore 0:
  9.9 30.4 all-gather.1
  107.7 19.4 reduce-scatter.1
where the time goes:
time: 226 us
  blocking collectives  79.7 us (35%)
  matrix products  70.9 us (31%)
  waiting for transfers between devices  50.7 us (22%)
  between operations  14.1 us (6%)
  other arithmetic  7.3 us (3%)
  local copies, waits for them, and re-layouts  2.62 us (1%)
    dot_general x1, matrix products, body(): jnp.einsum('kic,krc->ir', lax.all_gather(tensor_blocks, 'wide', axis=1, t...  67.1 us
    psum x1, blocking collectives, body(): lax.psum((jnp.dot(basis_rows, once.T, precision=hi), jnp.dot(once, once.T...  41.3 us
    psum x1, blocking collectives, body(): lax.psum((local_first, local_correlation), ('wide', 'narrow'))  38.5 us
    all_gather x1, waiting for transfers between devices, body(): lax.all_gather(tensor_blocks, 'wide', axis=1, tiled=True)  31.3 us
    reduce_scatter x1, waiting for transfers between devices, body(): lax.psum_scatter(partial_block, 'narrow', scatter_dimension=1, tiled=True)  19.4 us
  transfers between devices with their start and end apart: 2, of which 2 were waited for; matrix products, arithmetic and copies ran while one was open for 0% of the time, Pallas kernels for 0%

commit v1 on v0

--- a/solution.py
+++ b/solution.py
@@ -6,13 +6,22 @@
 N = 8192
 
 
+def doubled_up(x, axis, dim):
+    ways, here = (lax.axis_size(axis), lax.axis_index(axis))
+    grown, reach = (x, 1)
+    while reach < ways:
+        theirs = lax.ppermute(grown, axis, [(d, d ^ reach) for d in range(ways)])
+        mine_first = jnp.concatenate([grown, theirs], axis=dim)
+        theirs_first = jnp.concatenate([theirs, grown], axis=dim)
+        grown = jnp.where(here & reach == 0, mine_first, theirs_first)
+        reach = 2 * reach
+    return grown
+
+
 def body(coefficients, tensor_blocks, basis_rows):
     hi = lax.Precision.HIGHEST
     partial_block = jnp.einsum(
-        "kic,krc->ir",
-        lax.all_gather(tensor_blocks, "wide", axis=1, tiled=True),
-        coefficients,
-        precision=hi,
+        "kic,krc->ir", doubled_up(tensor_blocks, "wide", 1), coefficients, precision=hi
     )
     image = lax.psum_scatter(partial_block, "narrow", scatter_dimension=1, tiled=True)
     local_first = jnp.dot(basis_rows, image.T, precision=hi)

time: 226 us -> 236 us (1.044)
  waiting for transfers between devices: 50.7 us -> 57.1 us
  starting transfers between devices: 0.08 us -> 5.34 us
    ppermute x0 -> x3, waiting for transfers between devices: none -> 36.5 us  [doubled_up(): theirs = lax.ppermute(grown, axis, [(d, d ^ reach) for d in range(ways)])]
    all_gather x1 -> x0, waiting for transfers between devices: 31.3 us -> none  [body(): lax.all_gather(tensor_blocks, 'wide', axis=1, tiled=True)]
    ppermute x0 -> x3, starting transfers between devices: none -> 5.3 us  [doubled_up(): theirs = lax.ppermute(grown, axis, [(d, d ^ reach) for d in range(ways)])]
  transfers between devices with their start and end apart: 2 -> 4, of which waited for: 2 -> 4; matrix products, arithmetic and copies ran while one was open for 0% -> 0% of each run, Pallas kernels for 0% -> 0%
where the time goes in v1:
time: 236 us; the launch traced here: 235 us
  blocking collectives  79.9 us (34%)
  matrix products  69.2 us (29%)
  waiting for transfers between devices  57.1 us (24%)
  between operations  14.1 us (6%)
  other arithmetic  8.62 us (4%)
  starting transfers between devices  5.34 us (2%)
    dot_general x1, matrix products, body(): jnp.einsum('kic,krc->ir', doubled_up(tensor_blocks, 'wide', 1), coefficie...  65.4 us
    psum x1, blocking collectives, body(): lax.psum((jnp.dot(basis_rows, once.T, precision=hi), jnp.dot(once, once.T...  41.4 us
    psum x1, blocking collectives, body(): lax.psum((local_first, local_correlation), ('wide', 'narrow'))  38.5 us
    ppermute x3, waiting for transfers between devices, doubled_up(): theirs = lax.ppermute(grown, axis, [(d, d ^ reach) for d in range(ways)])  36.5 us
    reduce_scatter x1, waiting for transfers between devices, body(): lax.psum_scatter(partial_block, 'narrow', scatter_dimension=1, tiled=True)  20.6 us
    ppermute x3, starting transfers between devices, doubled_up(): theirs = lax.ppermute(grown, axis, [(d, d ^ reach) for d in range(ways)])  5.3 us
  transfers between devices with their start and end apart: 4, of which 4 were waited for; matrix products, arithmetic and copies ran while one was open for 0% of the time, Pallas kernels for 0%

profile of v1, /device:TPU:0, one launch (start us, length us, event | category | flops | bytes accessed | tf_op | source)
XLA Modules:
  0.0 235.0 jit_solution(1899170188064316248)
XLA Ops:
  7.2 0.6 collective-permute-start
  7.8 1.4 collective-permute-done
  9.2 1.2 maximum_select_fusion.5
  10.4 2.9 %collective-permute-start.1 = (f32[8,8,2048]{2,1,0:T(8,128)S(1)}, f32[8,8,2048]{2,1,0:T(8,128)S(1)}, u32[]{:S(2)}, u32[]{:S(2)}) collective-permute-start(f32[8,8,2048]{2,1,0:T(8,128)S(1)} %maximum_select_fusion.5), channel_id=1, source_target_pairs={{0,8},{4,12},{8,0},{12,4},{16,24},{20,28},{24,16},{28,20},{1,9},{5... | collective-permute-start | bytes 1572872 | tf_op jit(solution)/shard_map/ppermute | solution.py:13
  13.3 12.2 %collective-permute-done.1 = f32[8,8,2048]{2,1,0:T(8,128)S(1)} collective-permute-done((f32[8,8,2048]{2,1,0:T(8,128)S(1)}, f32[8,8,2048]{2,1,0:T(8,128)S(1)}, u32[]{:S(2)}, u32[]{:S(2)}) %collective-permute-start.1) | collective-permute-done | bytes 524320 | tf_op jit(solution)/shard_map/ppermute | solution.py:13
  25.6 1.8 collective-permute-start.2
  27.5 22.9 %collective-permute-done.2 = f32[8,16,2048]{2,1,0:T(8,128)S(1)} collective-permute-done((f32[8,16,2048]{2,1,0:T(8,128)S(1)}, f32[8,16,2048]{2,1,0:T(8,128)S(1)}, u32[]{:S(2)}, u32[]{:S(2)}) %collective-permute-start.2) | collective-permute-done | bytes 1048608 | tf_op jit(solution)/shard_map/ppermute | solution.py:13
  50.3 65.4 %fusion.6 = f32[32,1024]{1,0:T(8,128)} fusion(f32[8,1024,2048]{2,1,0:T(8,128)} %param.3, f32[8,16,2048]{2,1,0:T(8,128)S(1)} %collective-permute-done.2, f32[8,16,2048]{2,1,0:T(8,128)S(1)} %maximum_select_fusion.4, pred[]{:T(512)S(6)} %eq.9), kind=kOutput, calls=%fused_computation.7 | convolution fusion | flops 6444023808 | bytes 69337088 | tf_op jit(solution)/shard_map/kic,krc->ir/dot_general | solution.py:23
  115.7 0.2 fusion.15
  115.9 20.6 %reduce-scatter.2.cloned.1.call-done = f32[32,256]{1,0:T(8,128)} async-done(((f32[32,1024]{1,0:T(8,128)}), f32[32,256]{1,0:T(8,128)}) %reduce-scatter.2.cloned.1.call-update) | async-done | bytes 32784 | tf_op jit(solution)/shard_map/reduce_scatter | solution.py:26
  136.5 0.9 convolution_bitcast_fusion.1
  137.5 38.5 %psum.28 = f32[32,32]{0,1:T(8,128)S(1)} all-reduce(f32[32,32]{0,1:T(8,128)S(1)} %convolution_bitcast_fusion.1), channel_id=1, replica_groups=mesh['wide'=8,'narrow'=4] {'wide','narrow'}, use_global_device_ids=true, to_apply=%region_1.2 | all-reduce | flops 1024 | bytes 8192 | tf_op jit(solution)/shard_map/psum | solution.py:29
  175.9 0.9 convolution_subtract_fusion.1
  176.9 0.2 convolution_bitcast_fusion
  177.0 0.2 fusion.14
  177.2 41.4 %all-reduce = (f32[32,32]{0,1:T(8,128)S(1)}, f32[32,32]{0,1:T(8,128)S(1)}, f32[32,32]{1,0:T(8,128)S(1)}) all-reduce(f32[32,32]{0,1:T(8,128)S(1)} %convolution_bitcast_fusion, f32[32,32]{0,1:T(8,128)S(1)} %fusion.14, f32[32,32]{1,0:T(8,128)S(1)} %fusion.15), channel_id=1, replica_groups=mesh['wide'=8,'narrow'=4] {'wide','narrow'}, use_global_device_ids=true, to_apply=%region_3.4 | all-reduce | flops 3072 | bytes 24576 | tf_op jit(solution)/shard_map/psum | solution.py:31
  218.6 0.2 convolution_subtract_fusion
  218.7 0.7 copy.10
  219.7 0.2 fusion.7
  220.0 2.9 %cholesky.16 = f32[32,32]{1,0:T(8,128)S(1)} custom-call(f32[32,32]{1,0:T(8,128)S(1)} %fusion.12), custom_call_target="Cholesky" | custom-call | tf_op jit(solution)/shard_map/jit(cholesky)/cholesky | solution.py:39
  223.0 0.6 compare_reduce_fusion
  223.6 1.3 select_bitcast_fusion
  224.9 2.4 %custom-call.6 = f32[1,32,32]{1,2,0:T(8,128)S(1)} custom-call(f32[1,32,32]{2,1,0:T(8,128)S(1)} %get-tuple-element.9), custom_call_target="InvertDiagBlocksLowerTriangular" | custom-call | tf_op jit(solution)/shard_map/triangular_solve | solution.py:40
  227.3 0.9 fusion.10
  (11 shorter events, 0.6 us)
Async XLA Ops:
  7.2 108.6 %copy-start = (f32[32,256]{1,0:T(8,128)S(1)}, f32[32,256]{1,0:T(8,128)}, u32[]{:S(2)}) copy-start(f32[32,256]{1,0:T(8,128)} %param.5) | copy-start | bytes 98308
  7.2 129.3 %reduce-scatter.2.cloned.1.call-start = ((), (), s32[]{:S(2)}) async-start(), calls=%async_computation.1 | async-start | bytes 163840 | tf_op jit(solution)/shard_map/reduce_scatter | solution.py:26
  7.2 1.9 collective-permute-start
  10.4 15.1 %collective-permute-start.1 = (f32[8,8,2048]{2,1,0:T(8,128)S(1)}, f32[8,8,2048]{2,1,0:T(8,128)S(1)}, u32[]{:S(2)}, u32[]{:S(2)}) collective-permute-start(f32[8,8,2048]{2,1,0:T(8,128)S(1)} %maximum_select_fusion.5), channel_id=1, source_target_pairs={{0,8},{4,12},{8,0},{12,4},{16,24},{20,28},{24,16},{28,20},{1,9},{5... | collective-permute-start | bytes 1572872 | tf_op jit(solution)/shard_map/ppermute | solution.py:13
  25.6 24.7 %collective-permute-start.2 = (f32[8,16,2048]{2,1,0:T(8,128)S(1)}, f32[8,16,2048]{2,1,0:T(8,128)S(1)}, u32[]{:S(2)}, u32[]{:S(2)}) collective-permute-start(f32[8,16,2048]{2,1,0:T(8,128)S(1)} %maximum_select_fusion.4), channel_id=1, source_target_pairs={{0,16},{4,20},{8,24},{12,28},{16,0},{20,4},{24,8},{28,12},{1,17},{... | collective-permute-start | bytes 3145736 | tf_op jit(solution)/shard_map/ppermute | solution.py:13
Sparse Core Ops, SparseCore 0:
  115.8 20.6 reduce-scatter.1
